TPU v7x, 32 devices: a whole 2x2x4 slice. The times are simulated.
32 devices in a mesh: seq: 4 (over y, x), rep: 8 (over z, core).
Axes of the slice: x: 2, y: 2, z: 4, core: 2. Of those that a mesh axis runs over, the one named last changes fastest.
Arguments:
- tile_embed: bfloat16 [8, 4096, 768], P('rep', 'seq'), may hold values from -6 to 6
- tile_source: int32 [8, 4096], P('rep', 'seq'), may hold values from 0 to 4095, as said below
- slide_len: int32 [8], P('rep'), may hold values from 2048 to 4096
- grad_out: bfloat16 [8, 4096, 768], P('rep', 'seq'), may hold values from -6 to 6
- w_query: bfloat16 [768, 768], replicated, may hold values from -0.11727427342914273 to 0.11727427342914273
- w_key: bfloat16 [768, 768], replicated, may hold values from -0.11727427342914273 to 0.11727427342914273
- w_value: bfloat16 [768, 768], replicated, may hold values from -0.21875 to 0.21875
- w_out: bfloat16 [768, 768], replicated, may hold values from -0.21875 to 0.21875
Outputs:
- encoded: bfloat16 [8, 4096, 768], P('rep', 'seq')
- embed_grad: bfloat16 [8, 4096, 768], P('rep', 'seq')
- grad_query: float32 [768, 768], replicated
- grad_key: float32 [768, 768], replicated
- grad_value: float32 [768, 768], replicated
- grad_outproj: float32 [768, 768], replicated
Inputs may be any that keep to these rules, and one draw needn't show every extreme that they name: For each slide, tile_source is a permutation of 0 to 4095; each run of 1024 slide positions (aligned) takes exactly 1024 // (number of such runs) rows from each aligned run of 1024 rows of tile_embed.
All inputs are finite; a program needn't handle non-finite values.
Results may differ from a plain program's by a relative error of at most 0.0025.
The roundings to bfloat16 on the way count: a program that leaves them out, or rounds other values in their place, can miss the bound.
Values may be sent and summed in bfloat16 or wider, within the bound.
No kernel may reach another device: no remote copies, remote signals or barrier semaphores. Data moves between devices by JAX's collectives and lax.ppermute only.
A program may use at most 192 MiB of HBM per device.

v0:
```python
import jax
import jax.numpy as jnp
from jax import lax
from jax.sharding import PartitionSpec as P

HEADS = 16
SEG = 1024
RATE = 16
NEGATIVE = -1e30


def chosen(dilation, head_count):
    return jnp.arange(dilation)[:, None] == (jnp.arange(head_count) % dilation)[None, :]


def sparse_rows(dense, dilation):
    row_count, head_count, trailing = dense.shape
    blocks = dense.astype(jnp.float32).reshape(
        row_count // dilation, dilation, head_count, trailing
    )
    selected = chosen(dilation, head_count)[None, :, :, None]
    return jnp.sum(jnp.where(selected, blocks, jnp.float32(0.0)), axis=1)


def spread_rows(sparse, dilation, filler):
    row_count, head_count, trailing = sparse.shape
    selected = chosen(dilation, head_count)[None, :, :, None]
    spread = jnp.where(selected, sparse[:, None], jnp.float32(filler))
    return spread.reshape(row_count * dilation, head_count, trailing)


def product(pattern, left_side, right_side):
    return jnp.einsum(pattern, left_side, right_side, preferred_element_type=jnp.float32)


def masked_scores(queries, key_rows, key_ok, pieces, scaling):
    scores = product("nqd,nkd->nqk", queries, key_rows) * scaling
    return jnp.where(key_ok.reshape(pieces, 1, -1), scores, NEGATIVE)


def head_forward(queries, key_rows, values, key_ok, pieces, scaling):
    head_width = queries.shape[-1]
    queries = queries.reshape(pieces, -1, head_width)
    key_rows = key_rows.reshape(pieces, -1, head_width)
    values = values.reshape(pieces, -1, head_width)
    scores = masked_scores(queries, key_rows, key_ok, pieces, scaling)
    maxima = jnp.max(scores, axis=-1)
    weights = jnp.exp(scores - maxima[..., None])
    totals = jnp.sum(weights, axis=-1)
    numerator = product("nqk,nkd->nqd", weights.astype(jnp.bfloat16), values)
    return (numerator.reshape(-1, head_width), maxima.reshape(-1), totals.reshape(-1))


def split_pieces(arrays, pieces):
    return tuple((member.reshape(pieces, -1, member.shape[-1]) for member in arrays))


def score_terms(queries, key_rows, values, key_ok, log_total, upstream, deltas, pieces, scaling):
    scores = masked_scores(queries, key_rows, key_ok, pieces, scaling)
    probabilities = jnp.exp(scores - log_total.reshape(pieces, -1, 1))
    prob_grad = product("nqd,nkd->nqk", upstream, values)
    score_grad = (probabilities * (prob_grad - deltas.reshape(pieces, -1, 1))).astype(jnp.bfloat16)
    return (probabilities, score_grad)


def head_backward(queries, key_rows, values, key_ok, log_total, upstream, deltas, pieces, scaling):
    head_width = queries.shape[-1]
    queries, key_rows, values, upstream = split_pieces(
        (queries, key_rows, values, upstream), pieces
    )
    probabilities, score_grad = score_terms(
        queries, key_rows, values, key_ok, log_total, upstream, deltas, pieces, scaling
    )
    value_grad = product("nqk,nqd->nkd", probabilities.astype(jnp.bfloat16), upstream)
    query_grad = product("nqk,nkd->nqd", score_grad, key_rows) * scaling
    key_grad = product("nqk,nqd->nkd", score_grad, queries) * scaling
    return (
        query_grad.reshape(-1, head_width),
        key_grad.reshape(-1, head_width),
        value_grad.reshape(-1, head_width),
    )


def heads_map(function, arrays, pieces, scaling):
    transposed = tuple((jnp.moveaxis(member, 1, 0) for member in arrays))
    results = lax.map(lambda members: function(*members, pieces, scaling), transposed)
    return tuple((jnp.moveaxis(member, 0, 1) for member in results))


def merge_parts(local_part, remote, dilation):
    numer_local, max_local, total_local = local_part
    numer_far = spread_rows(remote[0], dilation, 0.0)
    max_far = spread_rows(remote[1][..., None], dilation, NEGATIVE)[..., 0]
    total_far = spread_rows(remote[2][..., None], dilation, 0.0)[..., 0]
    highest = jnp.maximum(max_local, max_far)
    weight_local = jnp.exp(max_local - highest)
    weight_far = jnp.exp(max_far - highest)
    combined = total_local * weight_local + total_far * weight_far
    output = (numer_local * weight_local[..., None] + numer_far * weight_far[..., None]) / combined[
        ..., None
    ]
    return (output, highest + jnp.log(combined))


def project(left_side, right_side):
    return jnp.dot(left_side, right_side, preferred_element_type=jnp.float32)


def per_device(tile_embed, tile_source, slide_len, grad_out, w_query, w_key, w_value, w_out):
    owned_rows = tile_embed[0]
    source = tile_source[0]
    row_count, features = owned_rows.shape
    stripes = lax.axis_size("seq")
    stripe = lax.axis_index("seq")
    portion = row_count // stripes
    owner_dev = source // row_count
    ordering = jnp.argsort(owner_dev, stable=True)
    wanted = (source % row_count)[ordering].reshape(stripes, portion)
    requested = lax.all_to_all(wanted, "seq", split_axis=0, concat_axis=0, tiled=True)
    picked = jnp.take(owned_rows, requested.reshape(-1), axis=0).reshape(stripes, portion, features)
    arrived = lax.all_to_all(picked, "seq", split_axis=0, concat_axis=0, tiled=True).reshape(
        row_count, features
    )
    embedded = jnp.zeros_like(arrived).at[ordering].set(arrived)
    length = slide_len[0]
    upstream_in = grad_out[0]
    head_dim = features // HEADS
    scaling = head_dim ** (-0.5)
    positions = stripe * row_count + jnp.arange(row_count)
    valid_rows = positions < length
    queries = project(embedded, w_query).astype(jnp.bfloat16).reshape(row_count, HEADS, head_dim)
    key_rows = project(embedded, w_key).astype(jnp.bfloat16).reshape(row_count, HEADS, head_dim)
    values = project(embedded, w_value).astype(jnp.bfloat16).reshape(row_count, HEADS, head_dim)
    local_ok = jnp.broadcast_to(valid_rows[:, None], (row_count, HEADS))
    local_part = heads_map(
        head_forward, (queries, key_rows, values, local_ok), row_count // SEG, scaling
    )
    sparse_q = sparse_rows(queries, RATE).astype(jnp.bfloat16)
    sparse_k = sparse_rows(key_rows, RATE).astype(jnp.bfloat16)
    sparse_v = sparse_rows(values, RATE).astype(jnp.bfloat16)
    near_count = sparse_k.shape[0]
    far_k, far_v = (
        lax.all_gather(sparse_k.reshape(near_count, features), "seq", axis=0, tiled=True),
        lax.all_gather(sparse_v.reshape(near_count, features), "seq", axis=0, tiled=True),
    )
    far_count = far_k.shape[0]
    far_k = far_k.reshape(far_count, HEADS, head_dim)
    far_v = far_v.reshape(far_count, HEADS, head_dim)
    sparse_pos = jnp.arange(far_count)[:, None] * RATE + (jnp.arange(HEADS) % RATE)[None, :]
    sparse_ok = sparse_pos < length
    remote = heads_map(head_forward, (sparse_q, far_k, far_v, sparse_ok), 1, scaling)
    output, log_total = merge_parts(local_part, remote, RATE)
    attended = (
        (output * valid_rows[:, None, None]).astype(jnp.bfloat16).reshape(row_count, features)
    )
    encoded = (embedded.astype(jnp.float32) + project(attended, w_out)).astype(jnp.bfloat16)
    upstream = (
        (project(upstream_in, w_out.T) * valid_rows[:, None])
        .astype(jnp.bfloat16)
        .reshape(row_count, HEADS, head_dim)
    )
    deltas = jnp.sum(upstream.astype(jnp.float32) * output, axis=-1)
    grad_outproj = jnp.einsum(
        "td,te->de", attended, upstream_in, preferred_element_type=jnp.float32
    )
    local_grads = heads_map(
        head_backward,
        (queries, key_rows, values, local_ok, log_total, upstream, deltas),
        row_count // SEG,
        scaling,
    )
    sparse_up = sparse_rows(upstream, RATE).astype(jnp.bfloat16)
    sparse_delta = sparse_rows(deltas[..., None], RATE)[..., 0]
    sparse_total = sparse_rows(log_total[..., None], RATE)[..., 0]
    remote_grads = heads_map(
        head_backward,
        (sparse_q, far_k, far_v, sparse_ok, sparse_total, sparse_up, sparse_delta),
        1,
        scaling,
    )
    key_back, value_back = (
        lax.psum_scatter(
            remote_grads[1].reshape(far_count, features), "seq", scatter_dimension=0, tiled=True
        ),
        lax.psum_scatter(
            remote_grads[2].reshape(far_count, features), "seq", scatter_dimension=0, tiled=True
        ),
    )
    key_back = key_back.reshape(near_count, HEADS, head_dim)
    value_back = value_back.reshape(near_count, HEADS, head_dim)
    query_far = remote_grads[0]
    query_grad = (
        (local_grads[0] + spread_rows(query_far, RATE, 0.0))
        .astype(jnp.bfloat16)
        .reshape(row_count, features)
    )
    key_grad = (
        (local_grads[1] + spread_rows(key_back, RATE, 0.0))
        .astype(jnp.bfloat16)
        .reshape(row_count, features)
    )
    value_grad = (
        (local_grads[2] + spread_rows(value_back, RATE, 0.0))
        .astype(jnp.bfloat16)
        .reshape(row_count, features)
    )
    embed_grad = upstream_in.astype(jnp.float32) + project(query_grad, w_query.T)
    embed_grad = embed_grad + project(key_grad, w_key.T)
    embed_grad = (embed_grad + project(value_grad, w_value.T)).astype(jnp.bfloat16)
    grad_query = jnp.einsum("td,te->de", embedded, query_grad, preferred_element_type=jnp.float32)
    grad_key = jnp.einsum("td,te->de", embedded, key_grad, preferred_element_type=jnp.float32)
    grad_value = jnp.einsum("td,te->de", embedded, value_grad, preferred_element_type=jnp.float32)
    summed = lax.psum((grad_query, grad_key, grad_value, grad_outproj), ("seq", "rep"))
    return (encoded[None], embed_grad[None], summed[0], summed[1], summed[2], summed[3])


def solution(mesh):
    return jax.shard_map(
        per_device,
        mesh=mesh,
        in_specs=(
            P("rep", "seq", None),
            P("rep", "seq"),
            P("rep"),
            P("rep", "seq", None),
            P(),
            P(),
            P(),
            P(),
        ),
        out_specs=(P("rep", "seq", None), P("rep", "seq", None), P(), P(), P(), P()),
        check_vma=False,
    )
```

profile of v0, /device:TPU:0, one launch (start us, length us, event | category | flops | bytes accessed | tf_op | source)
XLA Modules:
  0.0 939.3 jit_solution(3229480369411910893)
XLA Ops:
  8.0 4.4 sort.17
  12.4 4.5 gather_fusion
  16.9 9.7 %all_to_all.14 = s32[4,1,256]{2,1,0:T(1,128)S(1)} all-to-all(s32[4,1,256]{2,1,0:T(1,128)S(1)} %bitcast.389), channel_id=1, replica_groups=mesh['seq'=4,'rep'=8] {'seq'}, dimensions={0} | all-to-all | bytes 8192 | tf_op jit(solution)/shard_map/all_to_all | solution.py:119
  26.6 4.0 gather_fusion.1
  32.0 4.5 all-to-all-start.1
  38.3 2.7 multiply_convert_fusion.2
  43.2 7.8 reshape.434
  53.0 4.9 copy.100
  58.0 6.4 scatter_custom_fusion
  64.4 3.3 convolution_convert_fusion.2
  69.7 7.8 reshape.431
  77.5 3.2 convolution_convert_fusion.1
  82.9 7.8 reshape.432
  90.7 4.3 convolution_convert_fusion
  95.1 3.0 copy.88
  98.1 7.8 reshape.433
  105.9 14.5 %select_reduce_fusion = (bf16[64,16,48]{2,1,0:T(8,128)(2,1)}, bf16[64,16,48]{2,1,0:T(8,128)(2,1)S(1)}, bf16[64,16,48]{2,1,0:T(8,128)(2,1)S(1)}, bf16[64,16,48]{2,1,0:T(8,128)(2,1)}) fusion(f32[64,16,16,48]{3,2,1,0:T(8,128)} %reshape.434, pred[16,16]{1,0:T(8,128)(4,1)S(1)} %iota_compare_fusion, f32[64,16,16,48]{3,2,1,0:T(8,128)} %reshape.432, ...), kind=kLoop, calls=%fused_computation.133 | loop fusion | flops 6094848 | bytes 12976384 | tf_op jit(solution)/shard_map/reduce_sum | solution.py:22
  120.6 10.6 %all_gather.6 = bf16[256,768]{1,0:T(8,128)(2,1)S(1)} all-gather(bf16[64,768]{1,0:T(8,128)(2,1)S(1)} %convert_element_type.144), channel_id=1, replica_groups=mesh['seq'=4,'rep'=8] {'seq'}, dimensions={0}, use_global_device_ids=true | all-gather | bytes 491520 | tf_op jit(solution)/shard_map/all_gather | solution.py:143
  132.2 8.9 all_gather.7
  143.7 26.0 %while.57 = (s32[]{:T(128)}, f32[16,64,48]{1,2,0:T(8,128)S(1)}, f32[16,64]{1,0:T(8,128)S(1)}, f32[16,64]{1,0:T(8,128)S(1)}, pred[16,256]{1,0:T(8,128)(4,1)S(1)},...) while((s32[]{:T(128)}, f32[16,64,48]{1,2,0:T(8,128)S(1)}, ...), condition=%wide.region_12.13_spmd, body=%wide.region_9.12_spmd.sunk | while | flops 3260290 | bytes 374129 | solution.py:86
  175.9 3.2 copy.80
  179.0 3.2 copy.81
  182.2 3.1 copy.82
  187.5 142.6 %while.56 = (s32[]{:T(128)}, f32[16,1024,48]{1,2,0:T(8,128)}, f32[16,1024]{1,0:T(8,128)S(1)}, f32[16,1024]{1,0:T(8,128)S(1)}, pred[16,1024]{1,0:T(8,128)(4,1)S(1...) while((s32[]{:T(128)}, f32[16,1024,48]{1,2,0:T(8,128)}, ...), condition=%wide.region_5.6_spmd, body=%wide.region_2.5_spmd.sunk | while | flops 212858880 | bytes 30383244 | solution.py:86
  192.3 4.0 fusion.202
  201.2 4.0 fusion.202
  210.1 4.0 fusion.202
  219.0 4.0 fusion.202
  228.0 4.0 fusion.202
  236.9 4.0 fusion.202
  245.8 4.0 fusion.202
  254.7 4.0 fusion.202
  263.6 4.0 fusion.202
  272.5 4.0 fusion.202
  281.5 4.0 fusion.202
  290.4 4.0 fusion.202
  299.3 4.0 fusion.202
  308.2 4.0 fusion.202
  317.1 4.0 fusion.202
  326.0 4.0 fusion.202
  332.5 7.9 copy.83
  340.4 13.4 %multiply_convert_fusion.1 = (bf16[1024,16,48]{2,1,0:T(8,128)(2,1)}, f32[1024,16,48]{2,1,0:T(8,128)S(1)}) fusion(f32[1024]{0:T(1024)S(1)} %copy-done.34, f32[1024,16]{1,0:T(8,128)} %copy.97, f32[1024,16]{1,0:T(8,128)S(1)} %copy.96, f32[64,16,48]{2,1,0:T(8,128)S(1)} %copy.95, pred[1024,16]{1,0:T(8,128)(4,1)S(1)} %copy-done.19, f32[1024,16]{1,0:T(8,128)S(1)} %copy.93, ...), kind=kLoop, calls=%fused_computation.135 | loop fusion | flops 5505024 | bytes 8278016 | tf_op jit(solution)/shard_map/convert_element_type | solution.py:154
  357.3 98.4 %while.59 = (s32[]{:T(128)}, f32[16,64,48]{1,2,0:T(8,128)S(1)}, f32[16,256,48]{1,2,0:T(8,128)}, f32[16,256,48]{1,2,0:T(8,128)}, pred[16,256]{1,0:T(8,128)(4,1)},...) while((s32[]{:T(128)}, f32[16,64,48]{1,2,0:T(8,128)S(1)}, ...), condition=%wide.region_20.21_spmd, body=%wide.region_19.20_spmd.sunk | while | flops 7994370 | bytes 687741 | solution.py:86
  458.0 3.1 copy.99
  470.3 181.2 %while.58 = (s32[]{:T(128)}, f32[16,1024,48]{1,2,0:T(8,128)}, f32[16,1024,48]{1,2,0:T(8,128)}, f32[16,1024,48]{1,2,0:T(8,128)}, pred[16,1024]{1,0:T(8,128)(4,1)S...) while((s32[]{:T(128)}, f32[16,1024,48]{1,2,0:T(8,128)}, ...), condition=%wide.region_15.16_spmd, body=%wide.region_14.15_spmd.sunk | while | flops 513900544 | bytes 21337212 | solution.py:86
  490.3 2.7 fusion.222
  501.6 2.7 fusion.222
  524.3 2.7 fusion.222
  592.2 2.7 fusion.222
  651.8 7.9 copy.102
  659.6 7.8 copy.112
  667.5 7.9 copy.115
  675.3 5.5 copy.98
  680.8 4.2 fusion.114
  687.8 15.2 %fusion.110 = (bf16[1024,16,48]{2,1,0:T(8,128)(2,1)}, bf16[1024,16,48]{2,1,0:T(8,128)(2,1)}, bf16[1024,16,48]{2,1,0:T(8,128)(2,1)}) fusion(f32[16,1024,48]{2,0,1:T(8,128)} %copy.102, f32[64,16,48]{2,1,0:T(8,128)S(1)} %copy.110, pred[1024,16]{1,0:T(8,128)(4,1)} %copy.94, f32[64,16,48]{2,1,0:T(8,128)S(1)} %copy.113, f32[16,1024,48]{2,0,1:T(8,128)} %copy.112, ...), kind=kLoop, calls=%fused_computation.127 | loop fusion | flops 7077888 | bytes 14761984 | tf_op jit(solution)/shard_map/convert_element_type | solution.py:194
  703.0 5.5 copy.111
  708.5 4.2 fusion.130
  712.7 5.5 copy.114
  718.2 4.2 fusion.131
  722.5 4.4 copy.117
  727.0 4.2 fusion.132
  731.2 5.0 fusion.117
  742.9 179.8 %all-reduce.3.cloned.1.call-done = (f32[768,768]{1,0:T(8,128)}, f32[768,768]{1,0:T(8,128)}, f32[768,768]{1,0:T(8,128)}, f32[768,768]{1,0:T(8,128)}) async-done(((f32[768,768]{1,0:T(8,128)}, f32[768,768]{1,0:T(8,128)}, f32[768,768]{1,0:T(8,128)}, f32[768,768]{1,0:T(8,128)}), (f32[768,768]{1,0:T(8,128)}, f32[768,768]{1,0:T(8,128)}, f32[768,768]{1,0:T(8,128)}, ...) | async-done | bytes 9437200 | tf_op jit(solution)/shard_map/psum | solution.py:213
  922.7 3.4 copy.193
  (580 shorter events, 428.1 us)
Async XLA Ops:
  7.2 19.4 %copy-start = (bf16[1,1024,768]{2,1,0:T(8,128)(2,1)S(1)}, bf16[1,1024,768]{2,1,0:T(8,128)(2,1)}, u32[]{:S(2)}) copy-start(bf16[1,1024,768]{2,1,0:T(8,128)(2,1)} %param.16) | copy-start | bytes 4718596
  32.0 6.3 copy-start.13
  32.0 26.0 %all-to-all-start.1 = ((bf16[4,256,768]{2,1,0:T(8,128)(2,1)}), bf16[4,256,768]{2,1,0:T(8,128)(2,1)}, u32[]{:S(2)}, u32[]{:S(2)}) async-start(bf16[4,256,768]{2,1,0:T(8,128)(2,1)} %broadcast_select_fusion), calls=%async_computation.1 | async-start | bytes 3145728 | tf_op jit(solution)/shard_map/all_to_all | solution.py:121
  36.5 648.5 %reduce-scatter.7.cloned.1.call-start = ((), (), s32[]{:S(2)}) async-start(), calls=%async_computation.4 | async-start | bytes 983040
  37.8 0.6 copy-start.33
  41.0 12.0 %copy-start.4 = (bf16[1024,768]{0,1:T(8,128)(2,1)}, bf16[1024,768]{0,1:T(8,128)(2,1)S(1)}, u32[]{:S(2)}) copy-start(bf16[1024,768]{0,1:T(8,128)(2,1)S(1)} %multiply_convert_fusion.2) | copy-start | bytes 4718596
  51.2 0.6 copy-start.31
  52.1 5.8 copy-start.26
  64.4 3.3 copy-start.15
  80.7 10.1 %copy-start.6 = (bf16[1024,768]{0,1:T(8,128)(2,1)}, bf16[1024,768]{0,1:T(8,128)(2,1)S(1)}, u32[]{:S(2)}) copy-start(bf16[1024,768]{0,1:T(8,128)(2,1)S(1)} %convolution_convert_fusion.1) | copy-start | bytes 4718596
  131.2 12.4 %copy-start.35 = (f32[16,64]{1,0:T(8,128)S(1)}, f32[16,64]{1,0:T(8,128)}, u32[]{:S(2)}) copy-start(f32[16,64]{1,0:T(8,128)} %custom-call.7) | copy-start | bytes 12292
  169.6 3.2 copy-start.9
  169.6 3.2 copy-start.22
  169.7 9.4 copy-start.30
  173.8 5.2 copy-start.7
  179.0 3.2 copy-start.8
  182.2 3.2 copy-start.36
  182.2 5.2 copy-start.28
  182.2 5.2 copy-start.29
  187.5 142.6 %copy-start.24 = (f32[1024,16]{0,1:T(8,128)S(1)}, f32[1024,16]{0,1:T(8,128)}, u32[]{:S(2)}) copy-start(f32[1024,16]{0,1:T(8,128)} %broadcast_in_dim.318) | copy-start | bytes 196612
  187.5 142.6 %copy-start.25 = (f32[1024,16]{0,1:T(8,128)S(1)}, f32[1024,16]{0,1:T(8,128)}, u32[]{:S(2)}) copy-start(f32[1024,16]{0,1:T(8,128)} %broadcast_in_dim.325) | copy-start | bytes 196612
  187.5 142.6 %copy-start.27 = (pred[1024,16]{0,1:T(8,128)(4,1)S(1)}, pred[1024,16]{0,1:T(8,128)(4,1)}, u32[]{:S(2)}) copy-start(pred[1024,16]{0,1:T(8,128)(4,1)} %copy-done.26) | copy-start | bytes 49156
  189.3 1.9 copy-start.2
  198.2 1.9 copy-start.2
  207.1 1.9 copy-start.2
  216.1 1.9 copy-start.2
  225.0 1.9 copy-start.2
  233.9 1.9 copy-start.2
  242.8 1.9 copy-start.2
  251.7 1.9 copy-start.2
  260.6 1.9 copy-start.2
  269.6 1.9 copy-start.2
  278.5 1.9 copy-start.2
  287.4 1.9 copy-start.2
  296.3 1.9 copy-start.2
  305.2 1.9 copy-start.2
  314.1 1.9 copy-start.2
  323.0 1.9 copy-start.2
  332.5 7.9 copy-start.19
  332.5 7.9 copy-start.34
  340.4 13.4 %copy-start.3 = (bf16[1024,16,48]{2,1,0:T(8,128)(2,1)S(1)}, bf16[1024,16,48]{2,1,0:T(8,128)(2,1)}, u32[]{:S(2)}) copy-start(bf16[1024,16,48]{2,1,0:T(8,128)(2,1)} %copy.100) | copy-start | bytes 4718596
  353.8 2.8 copy-start.23
  353.8 3.0 copy-start.21
  353.8 3.1 copy-start.32
  357.2 100.8 %copy-start.5 = (bf16[1024,768]{0,1:T(8,128)(2,1)S(1)}, bf16[1024,768]{0,1:T(8,128)(2,1)}, u32[]{:S(2)}) copy-start(bf16[1024,768]{0,1:T(8,128)(2,1)} %copy-done.4) | copy-start | bytes 4718596
  458.0 228.4 %reduce-scatter.9.cloned.1.call-start = ((), (), s32[]{:S(2)}) async-start(), calls=%async_computation.5 | async-start | bytes 983040
  463.7 459.1 %all-reduce.3.cloned.1.call-start = ((), (), s32[]{:S(2)}) async-start(), calls=%async_computation.6 | async-start | bytes 18874368 | tf_op jit(solution)/shard_map/psum | solution.py:213
  675.3 5.5 copy-start.14
  703.0 5.5 copy-start.16
  731.2 5.0 copy-start.17
  731.2 5.0 copy-start.37
  736.2 1.9 copy-start.18
  736.2 2.5 copy-start.38
  738.8 1.5 copy-start.20
  922.7 3.4 copy-start.12
  926.1 2.5 copy-start.11
  928.6 2.5 copy-start.10
  928.6 3.9 copy-start.1
Sparse Core Ops, SparseCore 0:
  458.1 26.4 reduce-scatter.6
  488.0 26.1 reduce-scatter.8
  731.3 191.3 all-reduce.2
where the time goes:
time: 954 us; the launch traced here: 939 us
  matrix products  421 us (44%)
  local copies, waits for them, and re-layouts  215 us (23%)
  waiting for transfers between devices  180 us (19%)
  other arithmetic  71.3 us (7%)
  blocking collectives  29.2 us (3%)
  between operations  15.2 us (2%)
    dot_general x224, matrix products, product(): jnp.einsum(pattern, left_side, right_side, preferred_element_type=jnp.flo...  380 us
    psum x1, waiting for transfers between devices, per_device(): lax.psum((grad_query, grad_key, grad_value, grad_outproj), ('seq', 'rep'))  180 us
    while x9, local copies, waits for them, and re-layouts, heads_map(): lax.map(lambda members: function(*members, pieces, scaling), transposed)  34.5 us
    while x32, local copies, waits for them, and re-layouts  30.9 us
    convert_element_type x6, local copies, waits for them, and re-layouts, sparse_rows(): dense.astype(jnp.float32)  30.7 us
    dot_general x8, matrix products, project(): return jnp.dot(left_side, right_side, preferred_element_type=jnp.float32)  24 us
  transfers between devices with their start and end apart: 4, of which 1 were waited for; matrix products, arithmetic and copies ran while one was open for 27% of the time, Pallas kernels for 0%

commit v1 on v0

--- a/solution.py
+++ b/solution.py
@@ -210,7 +210,7 @@
     grad_query = jnp.einsum("td,te->de", embedded, query_grad, preferred_element_type=jnp.float32)
     grad_key = jnp.einsum("td,te->de", embedded, key_grad, preferred_element_type=jnp.float32)
     grad_value = jnp.einsum("td,te->de", embedded, value_grad, preferred_element_type=jnp.float32)
-    summed = lax.psum((grad_query, grad_key, grad_value, grad_outproj), ("seq", "rep"))
+    summed = lax.psum(lax.psum((grad_query, grad_key, grad_value, grad_outproj), "rep"), "seq")
     return (encoded[None], embed_grad[None], summed[0], summed[1], summed[2], summed[3])
 
 

time: 954 us -> 1150 us (1.21)
  waiting for transfers between devices: 180 us -> 377 us
    psum x1 -> x2, waiting for transfers between devices: 180 us -> 377 us  [the longest x1 196 us: per_device(): lax.psum((grad_query, grad_key, grad_value, grad_outproj), 'rep')]
  transfers between devices with their start and end apart: 4 -> 5, of which waited for: 1 -> 2; matrix products, arithmetic and copies ran while one was open for 27% -> 23% of each run, Pallas kernels for 0% -> 0%
where the time goes in v1:
time: 1150 us; the launch traced here: 1140 us
  matrix products  421 us (37%)
  waiting for transfers between devices  377 us (33%)
  local copies, waits for them, and re-layouts  215 us (19%)
  other arithmetic  71.3 us (6%)
  blocking collectives  29.2 us (3%)
  between operations  15.2 us (1%)
    dot_general x224, matrix products, product(): jnp.einsum(pattern, left_side, right_side, preferred_element_type=jnp.flo...  380 us
    psum x1, waiting for transfers between devices, per_device(): lax.psum((grad_query, grad_key, grad_value, grad_outproj), 'rep')  196 us
    psum x1, waiting for transfers between devices, per_device(): lax.psum(lax.psum((grad_query, grad_key, grad_value, grad_outproj), 'rep'...  181 us
    while x9, local copies, waits for them, and re-layouts, heads_map(): lax.map(lambda members: function(*members, pieces, scaling), transposed)  34.5 us
    while x32, local copies, waits for them, and re-layouts  31 us
    convert_element_type x6, local copies, waits for them, and re-layouts, sparse_rows(): dense.astype(jnp.float32)  30.7 us
    dot_general x8, matrix products, project(): return jnp.dot(left_side, right_side, preferred_element_type=jnp.float32)  24 us
  transfers between devices with their start and end apart: 5, of which 2 were waited for; matrix products, arithmetic and copies ran while one was open for 23% of the time, Pallas kernels for 0%

profile of v1, /device:TPU:0, one launch (start us, length us, event | category | flops | bytes accessed | tf_op | source)
XLA Modules:
  0.0 1136.3 jit_solution(5038618839337548659)
XLA Ops:
  8.0 4.4 sort.17
  12.4 4.5 gather_fusion
  16.9 9.7 all_to_all.14
  26.6 4.0 gather_fusion.1
  32.0 4.5 all-to-all-start.1
  38.4 2.7 multiply_convert_fusion.2
  43.4 7.8 reshape.434
  53.2 4.9 copy.100
  58.1 6.4 scatter_custom_fusion
  64.5 3.3 convolution_convert_fusion.2
  69.9 7.8 reshape.431
  77.6 3.2 convolution_convert_fusion.1
  83.0 7.8 reshape.432
  90.9 4.3 convolution_convert_fusion
  95.2 3.0 copy.88
  98.2 7.8 reshape.433
  106.0 14.5 %select_reduce_fusion = (bf16[64,16,48]{2,1,0:T(8,128)(2,1)}, bf16[64,16,48]{2,1,0:T(8,128)(2,1)S(1)}, bf16[64,16,48]{2,1,0:T(8,128)(2,1)S(1)}, bf16[64,16,48]{2,1,0:T(8,128)(2,1)}) fusion(f32[64,16,16,48]{3,2,1,0:T(8,128)} %reshape.434, pred[16,16]{1,0:T(8,128)(4,1)S(1)} %iota_compare_fusion, f32[64,16,16,48]{3,2,1,0:T(8,128)} %reshape.432, ...), kind=kLoop, calls=%fused_computation.133 | loop fusion | flops 6094848 | bytes 12976384 | tf_op jit(solution)/shard_map/reduce_sum | solution.py:22
  120.7 10.6 all_gather.6
  132.3 8.9 all_gather.7
  143.8 26.0 %while.57 = (s32[]{:T(128)}, f32[16,64,48]{1,2,0:T(8,128)S(1)}, f32[16,64]{1,0:T(8,128)S(1)}, f32[16,64]{1,0:T(8,128)S(1)}, pred[16,256]{1,0:T(8,128)(4,1)S(1)},...) while((s32[]{:T(128)}, f32[16,64,48]{1,2,0:T(8,128)S(1)}, ...), condition=%wide.region_12.13_spmd, body=%wide.region_9.12_spmd.sunk | while | flops 3260290 | bytes 374129 | solution.py:86
  176.0 3.2 copy.80
  179.2 3.2 copy.81
  182.4 3.2 copy.82
  187.6 142.7 %while.56 = (s32[]{:T(128)}, f32[16,1024,48]{1,2,0:T(8,128)}, f32[16,1024]{1,0:T(8,128)S(1)}, f32[16,1024]{1,0:T(8,128)S(1)}, pred[16,1024]{1,0:T(8,128)(4,1)S(1...) while((s32[]{:T(128)}, f32[16,1024,48]{1,2,0:T(8,128)}, ...), condition=%wide.region_5.6_spmd, body=%wide.region_2.5_spmd.sunk | while | flops 212858880 | bytes 30383244 | solution.py:86
  192.5 4.0 fusion.202
  201.4 4.0 fusion.202
  210.3 4.0 fusion.202
  219.2 4.0 fusion.202
  228.2 4.0 fusion.202
  237.1 4.0 fusion.202
  246.0 4.0 fusion.202
  254.9 4.0 fusion.202
  263.8 4.0 fusion.202
  272.7 4.0 fusion.202
  281.7 4.0 fusion.202
  290.6 4.0 fusion.202
  299.5 4.0 fusion.202
  308.4 4.0 fusion.202
  317.3 4.0 fusion.202
  326.2 4.0 fusion.202
  332.8 7.9 copy.83
  340.7 13.4 %multiply_convert_fusion.1 = (bf16[1024,16,48]{2,1,0:T(8,128)(2,1)}, f32[1024,16,48]{2,1,0:T(8,128)S(1)}) fusion(f32[1024]{0:T(1024)S(1)} %copy-done.34, f32[1024,16]{1,0:T(8,128)} %copy.97, f32[1024,16]{1,0:T(8,128)S(1)} %copy.96, f32[64,16,48]{2,1,0:T(8,128)S(1)} %copy.95, pred[1024,16]{1,0:T(8,128)(4,1)S(1)} %copy-done.19, f32[1024,16]{1,0:T(8,128)S(1)} %copy.93, ...), kind=kLoop, calls=%fused_computation.135 | loop fusion | flops 5505024 | bytes 8278016 | tf_op jit(solution)/shard_map/convert_element_type | solution.py:154
  357.5 98.4 %while.59 = (s32[]{:T(128)}, f32[16,64,48]{1,2,0:T(8,128)S(1)}, f32[16,256,48]{1,2,0:T(8,128)}, f32[16,256,48]{1,2,0:T(8,128)}, pred[16,256]{1,0:T(8,128)(4,1)},...) while((s32[]{:T(128)}, f32[16,64,48]{1,2,0:T(8,128)S(1)}, ...), condition=%wide.region_20.21_spmd, body=%wide.region_19.20_spmd.sunk | while | flops 7994370 | bytes 687741 | solution.py:86
  458.3 3.2 copy.99
  470.6 181.2 %while.58 = (s32[]{:T(128)}, f32[16,1024,48]{1,2,0:T(8,128)}, f32[16,1024,48]{1,2,0:T(8,128)}, f32[16,1024,48]{1,2,0:T(8,128)}, pred[16,1024]{1,0:T(8,128)(4,1)S...) while((s32[]{:T(128)}, f32[16,1024,48]{1,2,0:T(8,128)}, ...), condition=%wide.region_15.16_spmd, body=%wide.region_14.15_spmd.sunk | while | flops 513900544 | bytes 21337212 | solution.py:86
  479.2 2.7 fusion.222
  547.2 2.7 fusion.222
  637.8 2.7 fusion.222
  652.1 7.9 copy.102
  660.0 7.8 copy.112
  667.8 7.9 copy.115
  675.7 5.5 copy.98
  681.2 4.2 fusion.114
  688.2 15.2 %fusion.110 = (bf16[1024,16,48]{2,1,0:T(8,128)(2,1)}, bf16[1024,16,48]{2,1,0:T(8,128)(2,1)}, bf16[1024,16,48]{2,1,0:T(8,128)(2,1)}) fusion(f32[16,1024,48]{2,0,1:T(8,128)} %copy.102, f32[64,16,48]{2,1,0:T(8,128)S(1)} %copy.110, pred[1024,16]{1,0:T(8,128)(4,1)} %copy.94, f32[64,16,48]{2,1,0:T(8,128)S(1)} %copy.113, f32[16,1024,48]{2,0,1:T(8,128)} %copy.112, ...), kind=kLoop, calls=%fused_computation.127 | loop fusion | flops 7077888 | bytes 14761984 | tf_op jit(solution)/shard_map/convert_element_type | solution.py:194
  703.4 5.5 copy.111
  708.8 4.2 fusion.130
  713.1 5.5 copy.114
  718.6 4.2 fusion.131
  722.8 4.4 copy.117
  727.3 4.2 fusion.132
  731.6 195.8 %all-reduce.5.cloned.1.call-done = (f32[768,768]{1,0:T(8,128)}, f32[768,768]{1,0:T(8,128)}, f32[768,768]{1,0:T(8,128)}, f32[768,768]{1,0:T(8,128)}) async-done(((f32[768,768]{1,0:T(8,128)}, f32[768,768]{1,0:T(8,128)}, f32[768,768]{1,0:T(8,128)}, f32[768,768]{1,0:T(8,128)}), (f32[768,768]{1,0:T(8,128)}, f32[768,768]{1,0:T(8,128)}, f32[768,768]{1,0:T(8,128)}, ...) | async-done | bytes 9437200 | tf_op jit(solution)/shard_map/psum | solution.py:213
  927.5 5.0 fusion.117
  938.3 181.4 %all-reduce.7.cloned.1.call-done = (f32[768,768]{1,0:T(8,128)}, f32[768,768]{1,0:T(8,128)}, f32[768,768]{1,0:T(8,128)}, f32[768,768]{1,0:T(8,128)}) async-done(((f32[768,768]{1,0:T(8,128)}, f32[768,768]{1,0:T(8,128)}, f32[768,768]{1,0:T(8,128)}, f32[768,768]{1,0:T(8,128)}), (f32[768,768]{1,0:T(8,128)}, f32[768,768]{1,0:T(8,128)}, f32[768,768]{1,0:T(8,128)}, ...) | async-done | bytes 9437200 | tf_op jit(solution)/shard_map/psum | solution.py:213
  1119.8 3.4 copy.197
  (583 shorter events, 430.3 us)
Async XLA Ops:
  7.2 19.4 %copy-start = (bf16[1,1024,768]{2,1,0:T(8,128)(2,1)S(1)}, bf16[1,1024,768]{2,1,0:T(8,128)(2,1)}, u32[]{:S(2)}) copy-start(bf16[1,1024,768]{2,1,0:T(8,128)(2,1)} %param.16) | copy-start | bytes 4718596
  32.0 6.4 copy-start.13
  32.0 26.1 %all-to-all-start.1 = ((bf16[4,256,768]{2,1,0:T(8,128)(2,1)}), bf16[4,256,768]{2,1,0:T(8,128)(2,1)}, u32[]{:S(2)}, u32[]{:S(2)}) async-start(bf16[4,256,768]{2,1,0:T(8,128)(2,1)} %broadcast_select_fusion), calls=%async_computation.1 | async-start | bytes 3145728 | tf_op jit(solution)/shard_map/all_to_all | solution.py:121
  36.5 648.9 %reduce-scatter.7.cloned.1.call-start = ((), (), s32[]{:S(2)}) async-start(), calls=%async_computation.4 | async-start | bytes 983040
  37.8 0.6 copy-start.33
  41.1 12.0 %copy-start.4 = (bf16[1024,768]{0,1:T(8,128)(2,1)}, bf16[1024,768]{0,1:T(8,128)(2,1)S(1)}, u32[]{:S(2)}) copy-start(bf16[1024,768]{0,1:T(8,128)(2,1)S(1)} %multiply_convert_fusion.2) | copy-start | bytes 4718596
  51.3 0.6 copy-start.31
  52.3 5.8 copy-start.26
  64.5 3.3 copy-start.15
  80.8 10.0 copy-start.6
  131.4 12.4 %copy-start.35 = (f32[16,64]{1,0:T(8,128)S(1)}, f32[16,64]{1,0:T(8,128)}, u32[]{:S(2)}) copy-start(f32[16,64]{1,0:T(8,128)} %custom-call.7) | copy-start | bytes 12292
  169.8 3.2 copy-start.9
  169.8 3.1 copy-start.22
  169.8 9.4 copy-start.30
  173.9 5.2 copy-start.7
  179.2 3.2 copy-start.8
  182.4 3.2 copy-start.36
  182.4 5.3 copy-start.28
  182.4 5.3 copy-start.29
  187.6 142.7 %copy-start.24 = (f32[1024,16]{0,1:T(8,128)S(1)}, f32[1024,16]{0,1:T(8,128)}, u32[]{:S(2)}) copy-start(f32[1024,16]{0,1:T(8,128)} %broadcast_in_dim.318) | copy-start | bytes 196612
  187.6 142.7 %copy-start.25 = (f32[1024,16]{0,1:T(8,128)S(1)}, f32[1024,16]{0,1:T(8,128)}, u32[]{:S(2)}) copy-start(f32[1024,16]{0,1:T(8,128)} %broadcast_in_dim.325) | copy-start | bytes 196612
  187.6 142.7 %copy-start.27 = (pred[1024,16]{0,1:T(8,128)(4,1)S(1)}, pred[1024,16]{0,1:T(8,128)(4,1)}, u32[]{:S(2)}) copy-start(pred[1024,16]{0,1:T(8,128)(4,1)} %copy-done.26) | copy-start | bytes 49156
  189.5 1.9 copy-start.2
  198.4 1.9 copy-start.2
  207.3 1.9 copy-start.2
  216.2 1.9 copy-start.2
  225.2 1.9 copy-start.2
  234.1 1.9 copy-start.2
  243.0 1.9 copy-start.2
  251.9 1.9 copy-start.2
  260.8 1.9 copy-start.2
  269.7 1.9 copy-start.2
  278.7 1.9 copy-start.2
  287.6 1.9 copy-start.2
  296.5 1.9 copy-start.2
  305.4 1.9 copy-start.2
  314.3 1.9 copy-start.2
  323.2 1.9 copy-start.2
  332.7 7.9 copy-start.19
  332.7 7.9 copy-start.34
  340.7 13.4 %copy-start.3 = (bf16[1024,16,48]{2,1,0:T(8,128)(2,1)S(1)}, bf16[1024,16,48]{2,1,0:T(8,128)(2,1)}, u32[]{:S(2)}) copy-start(bf16[1024,16,48]{2,1,0:T(8,128)(2,1)} %copy.100) | copy-start | bytes 4718596
  354.1 2.8 copy-start.23
  354.1 3.0 copy-start.21
  354.1 3.1 copy-start.32
  357.5 100.8 %copy-start.5 = (bf16[1024,768]{0,1:T(8,128)(2,1)S(1)}, bf16[1024,768]{0,1:T(8,128)(2,1)}, u32[]{:S(2)}) copy-start(bf16[1024,768]{0,1:T(8,128)(2,1)} %copy-done.4) | copy-start | bytes 4718596
  458.2 228.5 %reduce-scatter.9.cloned.1.call-start = ((), (), s32[]{:S(2)}) async-start(), calls=%async_computation.5 | async-start | bytes 983040
  463.9 463.5 %all-reduce.5.cloned.1.call-start = ((), (), s32[]{:S(2)}) async-start(), calls=%async_computation.6 | async-start | bytes 18874368 | tf_op jit(solution)/shard_map/psum | solution.py:213
  675.7 5.5 copy-start.14
  703.3 5.5 copy-start.16
  731.6 388.2 %all-reduce.7.cloned.1.call-start = ((), (), s32[]{:S(2)}) async-start(), calls=%async_computation.7 | async-start | bytes 18874368 | tf_op jit(solution)/shard_map/psum | solution.py:213
  927.4 5.0 copy-start.17
  927.4 5.0 copy-start.37
  932.4 1.5 copy-start.18
  932.4 1.7 copy-start.38
  934.2 1.5 copy-start.20
  1119.8 3.4 copy-start.12
  1123.1 2.5 copy-start.11
  1125.6 2.5 copy-start.10
  1125.6 3.9 copy-start.1
Sparse Core Ops, SparseCore 0:
  458.4 26.4 reduce-scatter.6
  488.3 26.1 reduce-scatter.8
  731.7 195.6 all-reduce.4
  931.2 188.5 all-reduce.6
